TPU v7x, 32 devices: a whole 2x2x4 slice. The times are simulated.
32 devices in a mesh: bias: 2 (over x), ea: 16 (over z, y, core).
Axes of the slice: x: 2, y: 2, z: 4, core: 2. Of those that a mesh axis runs over, the one named last changes fastest.
Arguments:
- g_lesser: bfloat16 [512, 2, 256, 256], P(('bias', 'ea')), parts along dimension 0, may hold values from -6 to 6
- g_greater: bfloat16 [512, 2, 256, 256], P(('bias', 'ea')), parts along dimension 0, may hold values from -6 to 6
- g_free: bfloat16 [512, 2, 256, 256], P(('bias', 'ea')), parts along dimension 0, may hold values from -3 to 3
- coulomb: bfloat16 [256, 256], replicated, may hold values from -0.375 to 0.375
Outputs:
- g_new: bfloat16 [512, 2, 256, 256], P(('bias', 'ea')), parts along dimension 0
There are 2 independent parts, one for each index of `bias`. A program takes and returns all parts, laid end to end along the dimension named above; an argument that names none is the same for every part. Nothing has to cross between parts.
All inputs are finite; a program needn't handle non-finite values.
Results may differ from a plain program's by a relative error of at most 0.022.
Values may be sent and summed in bfloat16 or wider, within the bound.
A program may use at most 192 MiB of HBM per device.

v0:
```python
import math

import jax
import jax.numpy as jnp
from jax import lax
from jax.sharding import PartitionSpec as P

NE = 256


def dft_tables(length, count):
    freq = jnp.arange(length, dtype=jnp.int32)
    places = jnp.arange(count, dtype=jnp.int32)
    phase = freq[:, None] * places[None, :] % length
    angle = phase.astype(jnp.float32) * (2.0 * math.pi / length)
    cosine = jnp.cos(angle)
    sine = jnp.sin(angle)
    stacked = jnp.concatenate([cosine, sine], axis=0)
    upper = stacked.astype(jnp.bfloat16)
    lower = (stacked - upper.astype(jnp.float32)).astype(jnp.bfloat16)
    backward = jnp.concatenate([cosine.T, sine.T], axis=0)
    return (upper, lower, backward)


def forward(tables, block, sign):
    upper, lower = tables
    length = upper.shape[0] // 2
    real_part = block[:, 0].reshape(block.shape[0], -1)
    imag_part = block[:, 1].reshape(block.shape[0], -1)
    width = real_part.shape[1]
    joined = jnp.concatenate([real_part, imag_part], axis=1)
    result = jnp.dot(upper, joined, preferred_element_type=jnp.float32)
    result = result + jnp.dot(lower, joined, preferred_element_type=jnp.float32)
    cos_real = result[:length, :width]
    cos_imag = result[:length, width:]
    sin_real = result[length:, :width]
    sin_imag = result[length:, width:]
    return (cos_real - sign * sin_imag, cos_imag + sign * sin_real)


def inverse(backward, real_part, imag_part, scale):
    count = backward.shape[0] // 2
    width = real_part.shape[1]
    joined = jnp.concatenate([real_part, imag_part], axis=1)
    result = jnp.dot(
        backward, joined, precision=lax.Precision.HIGH, preferred_element_type=jnp.float32
    )
    cos_real = result[:count, :width]
    cos_imag = result[:count, width:]
    sin_real = result[count:, :width]
    sin_imag = result[count:, width:]
    return ((cos_real - sin_imag) * scale, (cos_imag + sin_real) * scale)


def complex_mul(left, right):
    return (left[0] * right[0] - left[1] * right[1], left[0] * right[1] + left[1] * right[0])


def restack(real_part, imag_part, shape):
    return jnp.stack([real_part.reshape(shape), imag_part.reshape(shape)], axis=1).astype(
        jnp.bfloat16
    )


def batched(left, right):
    return jnp.einsum("eij,ejk->eik", left, right, preferred_element_type=jnp.float32)


def per_device(g_lesser, g_greater, g_free, coulomb):
    length = 2 * NE
    upper, lower, backward = dft_tables(length, NE)
    tables = (upper, lower)
    scale = 1.0 / (length * NE)
    greater_t = jnp.swapaxes(g_greater, 2, 3)
    lesser_rows, greater_rows = (
        lax.all_to_all(g_lesser, "ea", split_axis=2, concat_axis=0, tiled=True),
        lax.all_to_all(greater_t, "ea", split_axis=2, concat_axis=0, tiled=True),
    )
    spec_lesser = forward(tables, lesser_rows, -1.0)
    element_shape = (NE, lesser_rows.shape[2], lesser_rows.shape[3])
    spec_greater = forward(tables, greater_rows, 1.0)
    joined = complex_mul(spec_lesser, spec_greater)
    polar_real, polar_imag = inverse(backward, joined[0], joined[1], scale)
    polar_rows = restack(polar_real, polar_imag, element_shape)
    polar = lax.all_to_all(polar_rows, "ea", split_axis=0, concat_axis=2, tiled=True)
    mixed_real = jnp.einsum(
        "eij,jk->eik", polar[:, 0], coulomb, preferred_element_type=jnp.float32
    ).astype(jnp.bfloat16)
    mixed_imag = jnp.einsum(
        "eij,jk->eik", polar[:, 1], coulomb, preferred_element_type=jnp.float32
    ).astype(jnp.bfloat16)
    square_real = batched(mixed_real, mixed_real) - batched(mixed_imag, mixed_imag)
    square_imag = batched(mixed_real, mixed_imag) + batched(mixed_imag, mixed_real)
    inner_real = (mixed_real.astype(jnp.float32) + square_real).astype(jnp.bfloat16)
    inner_imag = (mixed_imag.astype(jnp.float32) + square_imag).astype(jnp.bfloat16)
    screen_real = coulomb.astype(jnp.float32)[None] + jnp.einsum(
        "ij,ejk->eik", coulomb, inner_real, preferred_element_type=jnp.float32
    )
    screen_imag = jnp.einsum("ij,ejk->eik", coulomb, inner_imag, preferred_element_type=jnp.float32)
    screen = jnp.stack([screen_real, screen_imag], axis=1).astype(jnp.bfloat16)
    screen_rows = lax.all_to_all(screen, "ea", split_axis=2, concat_axis=0, tiled=True)
    spec_screen = forward(tables, screen_rows, -1.0)
    folded = complex_mul(spec_lesser, spec_screen)
    sigma_real, sigma_imag = inverse(backward, folded[0], folded[1], scale)
    sigma_rows = restack(sigma_real, sigma_imag, element_shape)
    sigma = lax.all_to_all(sigma_rows, "ea", split_axis=0, concat_axis=2, tiled=True)
    free_real = g_free[:, 0]
    free_imag = g_free[:, 1]
    right_real = (batched(sigma[:, 0], free_real) - batched(sigma[:, 1], free_imag)).astype(
        jnp.bfloat16
    )
    right_imag = (batched(sigma[:, 0], free_imag) + batched(sigma[:, 1], free_real)).astype(
        jnp.bfloat16
    )
    out_real = (
        free_real.astype(jnp.float32)
        + batched(free_real, right_real)
        - batched(free_imag, right_imag)
    )
    out_imag = (
        free_imag.astype(jnp.float32)
        + batched(free_real, right_imag)
        + batched(free_imag, right_real)
    )
    return jnp.stack([out_real, out_imag], axis=1).astype(jnp.bfloat16)


def solution(mesh):
    return jax.shard_map(
        per_device,
        mesh=mesh,
        in_specs=(
            P(("bias", "ea"), None, None, None),
            P(("bias", "ea"), None, None, None),
            P(("bias", "ea"), None, None, None),
            P(),
        ),
        out_specs=P(("bias", "ea"), None, None, None),
        check_vma=False,
    )
```

profile of v0, /device:TPU:13, one launch (start us, length us, event | category | flops | bytes accessed | tf_op | source)
XLA Modules:
  0.0 770.7 jit_solution(499210198396497137)
XLA Ops:
  0.0 11.1 %copy.96 = bf16[16,2,256,256]{2,1,0,3:T(2,128)(2,1)} copy(bf16[16,2,256,256]{3,2,1,0:T(8,128)(2,1)} %param.5) | data formatting | bytes 8388608 | tf_op args[1]
  11.1 6.5 all-to-all-start.1
  17.7 6.5 copy.92
  24.2 85.9 %all-to-all-done.1 = bf16[16,2,256,256]{3,1,0,2:T(2,128)(2,1)} async-done(((bf16[16,2,256,256]{3,1,0,2:T(2,128)(2,1)}), bf16[16,2,256,256]{3,1,0,2:T(2,128)(2,1)}, u32[]{:S(2)}, u32[]{:S(2)}) %all-to-all-start.1) | async-done | bytes 4194336 | tf_op jit(solution)/shard_map/all_to_all | solution.py:77
  110.1 5.1 all-to-all-start
  115.2 2.1 fusion.67
  117.3 2.9 fusion.69
  120.2 4.6 copy.97
  125.8 1.0 copy.136
  126.7 1.0 copy.137
  128.2 13.1 %fusion.79 = f32[1024,8192]{1,0:T(8,128)} fusion(bf16[256,8192]{1,0:T(8,128)(2,1)S(1)} %constant_dynamic-update-slice_fusion.2, f32[512,256]{1,0:T(8,128)S(1)} %get-tuple-element.20, f32[512,256]{1,0:T(8,128)S(1)} %get-tuple-element.21), kind=kOutput, calls=%fused_computation.124 | convolution fusion | flops 4296015872 | bytes 38797312 | tf_op jit(solution)/shard_map/dot_general | solution.py:32
  141.3 25.0 %convolution_add_fusion.1 = f32[1024,8192]{1,0:T(8,128)} fusion(f32[1024,8192]{1,0:T(8,128)} %fusion.79, bf16[256,8192]{1,0:T(8,128)(2,1)S(1)} %constant_dynamic-update-slice_fusion.2, f32[512,256]{1,0:T(8,128)S(1)} %get-tuple-element.20, f32[512,256]{1,0:T(8,128)} %copy-done.2), kind=kOutput, calls=%fused_computation.1 | convolution fusion | flops 4304666624 | bytes 72351744 | tf_op jit(solution)/shard_map/dot_general | solution.py:33
  166.3 41.2 %all-to-all-done = bf16[16,2,256,256]{3,0,1,2:T(8,128)(2,1)} async-done(((bf16[16,2,256,256]{3,0,1,2:T(8,128)(2,1)}), bf16[16,2,256,256]{3,0,1,2:T(8,128)(2,1)}, u32[]{:S(2)}, u32[]{:S(2)}) %all-to-all-start) | async-done | bytes 4194336 | tf_op jit(solution)/shard_map/all_to_all | solution.py:76
  207.5 5.0 copy.94
  212.9 0.9 copy.134
  214.0 1.0 copy.135
  215.3 13.1 %fusion.81 = f32[1024,8192]{1,0:T(8,128)} fusion(bf16[256,8192]{1,0:T(8,128)(2,1)S(1)} %constant_dynamic-update-slice_fusion, f32[512,256]{1,0:T(8,128)S(1)} %get-tuple-element.20, f32[512,256]{1,0:T(8,128)S(1)} %copy-done.3), kind=kOutput, calls=%fused_computation.125 | convolution fusion | flops 4296015872 | bytes 38797312 | tf_op jit(solution)/shard_map/dot_general | solution.py:32
  228.3 24.9 %convolution_add_fusion.2 = f32[1024,8192]{1,0:T(8,128)} fusion(f32[1024,8192]{1,0:T(8,128)} %fusion.81, bf16[256,8192]{1,0:T(8,128)(2,1)S(1)} %constant_dynamic-update-slice_fusion, f32[512,256]{1,0:T(8,128)S(1)} %get-tuple-element.20, f32[512,256]{1,0:T(8,128)} %copy-done.2), kind=kOutput, calls=%fused_computation.2 | convolution fusion | flops 4304666624 | bytes 72351744 | tf_op jit(solution)/shard_map/dot_general | solution.py:33
  253.2 31.7 %multiply_subtract_fusion.1 = (f32[512,4096]{1,0:T(8,128)}, f32[512,4096]{1,0:T(8,128)}, f32[512,4096]{1,0:T(8,128)}) fusion(f32[1024,8192]{1,0:T(8,128)} %convolution_add_fusion.1, f32[1024,8192]{1,0:T(8,128)} %convolution_add_fusion.2), kind=kLoop, calls=%fused_computation.24 | loop fusion | flops 18874368 | bytes 92274688 | tf_op jit(solution)/shard_map/sub | solution.py:56
  284.9 22.0 %multiply_add_fusion.1 = f32[512,4096]{1,0:T(8,128)} fusion(f32[512,4096]{1,0:T(8,128)} %get-tuple-element.7, f32[512,4096]{1,0:T(8,128)} %get-tuple-element.6, f32[1024,8192]{1,0:T(8,128)} %convolution_add_fusion.1), kind=kLoop, calls=%fused_computation.23 | loop fusion | flops 10485760 | bytes 58720256 | tf_op jit(solution)/shard_map/add | solution.py:56
  306.9 19.5 %fusion = f32[512,8192]{1,0:T(8,128)} fusion(f32[512,4096]{1,0:T(8,128)} %multiply_add_fusion.1, f32[512,4096]{1,0:T(8,128)} %get-tuple-element.5, f32[256,512]{1,0:T(8,128)S(1)} %copy-done.6, f32[256,512]{1,0:T(8,128)S(1)} %copy-done.8), kind=kOutput, calls=%fused_computation.3 | convolution fusion | flops 12889358336 | bytes 34603008 | tf_op jit(solution)/shard_map/dot_general | solution.py:45
  326.4 6.7 fusion.19
  334.4 2.4 pad_maximum_fusion
  336.8 4.9 all-to-all-start.2
  341.8 92.4 %all-to-all-done.2 = bf16[256,2,16,256]{3,2,1,0:T(8,128)(2,1)} async-done(((bf16[256,2,16,256]{3,2,1,0:T(8,128)(2,1)}), bf16[256,2,16,256]{3,2,1,0:T(8,128)(2,1)}, u32[]{:S(2)}, u32[]{:S(2)}) %all-to-all-start.2) | async-done | bytes 4194336 | tf_op jit(solution)/shard_map/all_to_all | solution.py:85
  434.2 2.7 copy.101
  438.4 2.7 fusion.88
  441.0 2.8 fusion.89
  443.8 6.4 convert_bitcast_fusion
  450.2 6.4 fusion.42
  456.6 4.6 pad_maximum_fusion.1
  461.2 7.9 %copy.104 = bf16[16,2,256,256]{3,0,1,2:T(8,128)(2,1)} copy(bf16[16,2,256,256]{2,3,0,1:T(8,128)(2,1)} %pad_maximum_fusion.1) | data formatting | bytes 8388608 | tf_op jit(solution)/shard_map/stack | solution.py:100
  469.1 97.2 %all_to_all.90 = bf16[16,2,256,256]{3,0,1,2:T(8,128)(2,1)S(1)} all-to-all(bf16[16,2,256,256]{3,0,1,2:T(8,128)(2,1)} %copy.104), channel_id=1, replica_groups=mesh['bias'=2,'ea'=16] {'ea'}, dimensions={2} | all-to-all | bytes 8388608 | tf_op jit(solution)/shard_map/all_to_all | solution.py:101
  566.3 2.9 copy.106
  569.5 0.9 copy.140
  570.7 1.0 copy.141
  571.9 13.1 %fusion.77 = f32[1024,8192]{1,0:T(8,128)} fusion(bf16[256,8192]{1,0:T(8,128)(2,1)S(1)} %constant_dynamic-update-slice_fusion.4, f32[512,256]{1,0:T(8,128)S(1)} %get-tuple-element.20, f32[512,256]{1,0:T(8,128)S(1)} %copy-done.4), kind=kOutput, calls=%fused_computation.123 | convolution fusion | flops 4296015872 | bytes 38797312 | tf_op jit(solution)/shard_map/dot_general | solution.py:32
  585.1 24.8 %convolution_add_fusion = f32[1024,8192]{1,0:T(8,128)} fusion(f32[1024,8192]{1,0:T(8,128)} %fusion.77, bf16[256,8192]{1,0:T(8,128)(2,1)S(1)} %constant_dynamic-update-slice_fusion.4, f32[512,256]{1,0:T(8,128)S(1)} %get-tuple-element.20, f32[512,256]{1,0:T(8,128)} %copy-done.2), kind=kOutput, calls=%fused_computation | convolution fusion | flops 4304666624 | bytes 72351744 | tf_op jit(solution)/shard_map/dot_general | solution.py:33
  609.9 23.8 %multiply_subtract_fusion = (f32[512,4096]{1,0:T(8,128)}, f32[512,4096]{1,0:T(8,128)}) fusion(f32[512,4096]{1,0:T(8,128)} %get-tuple-element.7, f32[512,4096]{1,0:T(8,128)} %get-tuple-element.6, f32[1024,8192]{1,0:T(8,128)} %convolution_add_fusion), kind=kLoop, calls=%fused_computation.22 | loop fusion | flops 20971520 | bytes 67108864 | tf_op jit(solution)/shard_map/sub | solution.py:56
  633.7 19.8 %fusion.4 = f32[512,8192]{1,0:T(8,128)} fusion(f32[512,4096]{1,0:T(8,128)} %get-tuple-element.9, f32[512,4096]{1,0:T(8,128)} %get-tuple-element.8, f32[256,512]{1,0:T(8,128)S(1)} %copy-done.7, f32[256,512]{1,0:T(8,128)S(1)} %copy-done.9), kind=kOutput, calls=%fused_computation.7 | convolution fusion | flops 12889358336 | bytes 34603008 | tf_op jit(solution)/shard_map/dot_general | solution.py:45
  653.5 6.7 fusion.15
  661.8 97.5 %all_to_all.91 = bf16[256,2,16,256]{3,2,1,0:T(8,128)(2,1)S(1)} all-to-all(bf16[256,2,16,256]{3,2,1,0:T(8,128)(2,1)S(1)} %pad_maximum_fusion.2), channel_id=1, replica_groups=mesh['bias'=2,'ea'=16] {'ea'}, dimensions={0} | all-to-all | bytes 8388608 | tf_op jit(solution)/shard_map/all_to_all | solution.py:106
  759.9 1.6 copy-done
  763.7 0.7 subtract_convert_fusion
  764.4 0.7 fusion.30
  765.8 0.9 fusion.43
  766.7 0.9 fusion.39
  768.1 2.3 copy.119
  (43 shorter events, 11.0 us)
Async XLA Ops:
  11.1 99.0 %all-to-all-start.1 = ((bf16[16,2,256,256]{3,1,0,2:T(2,128)(2,1)}), bf16[16,2,256,256]{3,1,0,2:T(2,128)(2,1)}, u32[]{:S(2)}, u32[]{:S(2)}) async-start(bf16[16,2,256,256]{3,1,0,2:T(2,128)(2,1)} %bitcast.181), calls=%async_computation.1 | async-start | bytes 8388608 | tf_op jit(solution)/shard_map/all_to_all | solution.py:77
  110.1 97.4 %all-to-all-start = ((bf16[16,2,256,256]{3,0,1,2:T(8,128)(2,1)}), bf16[16,2,256,256]{3,0,1,2:T(8,128)(2,1)}, u32[]{:S(2)}, u32[]{:S(2)}) async-start(bf16[16,2,256,256]{3,0,1,2:T(8,128)(2,1)} %copy.92), calls=%async_computation | async-start | bytes 8388608 | tf_op jit(solution)/shard_map/all_to_all | solution.py:76
  117.3 10.9 %copy-start.2 = (f32[512,256]{1,0:T(8,128)}, f32[512,256]{1,0:T(8,128)S(1)}, u32[]{:S(2)}) copy-start(f32[512,256]{1,0:T(8,128)S(1)} %get-tuple-element.21) | copy-start | bytes 1572868
  214.0 1.2 copy-start.3
  284.9 22.0 %copy-start.6 = (f32[256,512]{1,0:T(8,128)S(1)}, f32[256,512]{1,0:T(8,128)}, u32[]{:S(2)}) copy-start(f32[256,512]{1,0:T(8,128)} %get-tuple-element.22) | copy-start | bytes 1572868
  284.9 22.0 %copy-start.8 = (f32[256,512]{1,0:T(8,128)S(1)}, f32[256,512]{1,0:T(8,128)}, u32[]{:S(2)}) copy-start(f32[256,512]{1,0:T(8,128)} %get-tuple-element.23) | copy-start | bytes 1572868
  336.8 4.9 copy-start.5
  336.8 97.4 %all-to-all-start.2 = ((bf16[256,2,16,256]{3,2,1,0:T(8,128)(2,1)}), bf16[256,2,16,256]{3,2,1,0:T(8,128)(2,1)}, u32[]{:S(2)}, u32[]{:S(2)}) async-start(bf16[256,2,16,256]{3,2,1,0:T(8,128)(2,1)} %pad_maximum_fusion), calls=%async_computation.2 | async-start | bytes 8388608 | tf_op jit(solution)/shard_map/all_to_all | solution.py:85
  438.3 2.7 copy-start.1
  570.7 1.2 copy-start.4
  609.9 23.8 %copy-start.7 = (f32[256,512]{1,0:T(8,128)S(1)}, f32[256,512]{1,0:T(8,128)}, u32[]{:S(2)}) copy-start(f32[256,512]{1,0:T(8,128)} %get-tuple-element.22) | copy-start | bytes 1572868
  609.9 23.8 %copy-start.9 = (f32[256,512]{1,0:T(8,128)S(1)}, f32[256,512]{1,0:T(8,128)}, u32[]{:S(2)}) copy-start(f32[256,512]{1,0:T(8,128)} %get-tuple-element.23) | copy-start | bytes 1572868
  759.3 2.2 copy-start
where the time goes:
time: 776 us; the launch traced here: 771 us
  waiting for transfers between devices  219 us (28%)
  blocking collectives  195 us (25%)
  matrix products  179 us (23%)
  other arithmetic  104 us (13%)
  local copies, waits for them, and re-layouts  56.6 us (7%)
  starting transfers between devices  16.5 us (2%)
    all_to_all x1, blocking collectives, per_device(): lax.all_to_all(sigma_rows, 'ea', split_axis=0, concat_axis=2, tiled=True)  97.5 us
    all_to_all x1, blocking collectives, per_device(): lax.all_to_all(screen, 'ea', split_axis=2, concat_axis=0, tiled=True)  97.2 us
    all_to_all x1, waiting for transfers between devices, per_device(): lax.all_to_all(polar_rows, 'ea', split_axis=0, concat_axis=2, tiled=True)  92.4 us
    all_to_all x1, waiting for transfers between devices, per_device(): lax.all_to_all(greater_t, 'ea', split_axis=2, concat_axis=0, tiled=True)  85.9 us
    dot_general x3, matrix products, forward(): result = result + jnp.dot(lower, joined, preferred_element_type=jnp.float32)  74.7 us
    sub x2, other arithmetic, complex_mul(): left[0] * right[0] - left[1] * right[1]  55.5 us
    all_to_all x1, waiting for transfers between devices, per_device(): lax.all_to_all(g_lesser, 'ea', split_axis=2, concat_axis=0, tiled=True)  41.2 us
    dot_general x3, matrix products, forward(): result = jnp.dot(upper, joined, preferred_element_type=jnp.float32)  39.4 us
  transfers between devices with their start and end apart: 3, of which 3 were waited for; matrix products, arithmetic and copies ran while one was open for 7% of the time, Pallas kernels for 0%

commit v1 on v0

--- a/solution.py
+++ b/solution.py
@@ -1,8 +1,12 @@
+import functools
 import math
 
 import jax
 import jax.numpy as jnp
+import numpy as np
 from jax import lax
+from jax.experimental import pallas as pl
+from jax.experimental.pallas import tpu as pltpu
 from jax.sharding import PartitionSpec as P
 
 NE = 256
@@ -66,7 +70,29 @@
     return jnp.einsum("eij,ejk->eik", left, right, preferred_element_type=jnp.float32)
 
 
-def per_device(g_lesser, g_greater, g_free, coulomb):
+def dyson(sigma_real, sigma_imag, g_free):
+    free_real = g_free[:, 0]
+    free_imag = g_free[:, 1]
+    right_real = (batched(sigma_real, free_real) - batched(sigma_imag, free_imag)).astype(
+        jnp.bfloat16
+    )
+    right_imag = (batched(sigma_real, free_imag) + batched(sigma_imag, free_real)).astype(
+        jnp.bfloat16
+    )
+    out_real = (
+        free_real.astype(jnp.float32)
+        + batched(free_real, right_real)
+        - batched(free_imag, right_imag)
+    )
+    out_imag = (
+        free_imag.astype(jnp.float32)
+        + batched(free_real, right_imag)
+        + batched(free_imag, right_real)
+    )
+    return jnp.stack([out_real, out_imag], axis=1).astype(jnp.bfloat16)
+
+
+def plain(g_lesser, g_greater, g_free, coulomb):
     length = 2 * NE
     upper, lower, backward = dft_tables(length, NE)
     tables = (upper, lower)
@@ -104,30 +130,225 @@
     sigma_real, sigma_imag = inverse(backward, folded[0], folded[1], scale)
     sigma_rows = restack(sigma_real, sigma_imag, element_shape)
     sigma = lax.all_to_all(sigma_rows, "ea", split_axis=0, concat_axis=2, tiled=True)
-    free_real = g_free[:, 0]
-    free_imag = g_free[:, 1]
-    right_real = (batched(sigma[:, 0], free_real) - batched(sigma[:, 1], free_imag)).astype(
-        jnp.bfloat16
-    )
-    right_imag = (batched(sigma[:, 0], free_imag) + batched(sigma[:, 1], free_real)).astype(
-        jnp.bfloat16
-    )
-    out_real = (
-        free_real.astype(jnp.float32)
-        + batched(free_real, right_real)
-        - batched(free_imag, right_imag)
-    )
-    out_imag = (
-        free_imag.astype(jnp.float32)
-        + batched(free_real, right_imag)
-        + batched(free_imag, right_real)
-    )
-    return jnp.stack([out_real, out_imag], axis=1).astype(jnp.bfloat16)
+    return dyson(sigma[:, 0], sigma[:, 1], g_free)
+
+
+MESH = pl.DeviceIdType.MESH
+CHUNKS = 4
+VMEM_BYTES = 60 * 1024 * 1024
+
+
+def transform_table(count):
+    length = 2 * count
+    phase = np.arange(length)[:, None] * np.arange(count)[None, :] % length
+    angle = phase * (2.0 * math.pi / length)
+    cosine, sine = np.cos(angle), np.sin(angle)
+    return np.block([[cosine, sine], [-sine, cosine]]).astype(np.float32)
+
+
+def greet(n):
+    me = lax.axis_index("ea")
+    barrier = pltpu.get_barrier_semaphore()
+
+    def hello(k, carry):
+        pl.semaphore_signal(
+            barrier, inc=1, device_id={"ea": lax.rem(me + k, n)}, device_id_type=MESH
+        )
+        return carry
+
+    lax.fori_loop(1, n, hello, 0)
+    pl.semaphore_wait(barrier, n - 1)
+
+
+def exchange_kernel(
+    n, count, first, scale, *refs
+):
+    if first:
+        (lesser, other, table, table_t, volts, out, kept,
+         lesser_buf, other_buf, folded, in_send, in_recv, out_send, out_recv, own_in, own_out, keep) = refs
+        streams = ((lesser, lesser_buf), (other, other_buf))
+    else:
+        (kept, other, table, table_t, out,
+         lesser_buf, other_buf, folded, in_send, in_recv, out_send, out_recv, own_in, own_out, keep) = refs
+        streams = ((other, other_buf),)
+    me = lax.axis_index("ea")
+    rows = folded.shape[1]
+    each = count // n
+    group = rows // CHUNKS
+
+    def incoming(s, q, k):
+        peer = lax.rem(me + k, n)
+        source, target = streams[s]
+        return pltpu.make_async_remote_copy(
+            src_ref=source.at[:, pl.ds(peer * rows + q * group, group)],
+            dst_ref=target.at[:, pl.ds(q * group, group), pl.ds(me * each, each)],
+            send_sem=in_send.at[s, q, k],
+            recv_sem=in_recv.at[s, q, k],
+            device_id={"ea": peer},
+            device_id_type=MESH,
+        )
+
+    def outgoing(q, k):
+        peer = lax.rem(me + k, n)
+        return pltpu.make_async_remote_copy(
+            src_ref=folded.at[:, pl.ds(q * group, group), pl.ds(peer * each, each)],
+            dst_ref=out.at[:, pl.ds(me * rows + q * group, group)],
+            send_sem=out_send.at[q, k],
+            recv_sem=out_recv.at[q, k],
+            device_id={"ea": peer},
+            device_id_type=MESH,
+        )
+
+    def own_incoming(s):
+        source, target = streams[s]
+        return pltpu.make_async_copy(
+            source.at[:, pl.ds(me * rows, rows)],
+            target.at[:, :, pl.ds(me * each, each)],
+            own_in.at[s],
+        )
+
+    if not first:
+        pltpu.make_async_copy(kept, lesser_buf, keep).start()
+    for s in range(len(streams)):
+        own_incoming(s).start()
+    greet(n)
+
+    def send_chunk(q, carry):
+        for s in range(len(streams)):
+            def send_one(k, inner):
+                incoming(s, q, k).start()
+                return inner
+            lax.fori_loop(1, n, send_one, 0)
+        return carry
+
+    lax.fori_loop(0, CHUNKS, send_chunk, 0)
+    for s in range(len(streams)):
+        own_incoming(s).wait()
+    if not first:
+        pltpu.make_async_copy(kept, lesser_buf, keep).wait()
+
+    length = 2 * count
+
+    def fold(row, carry):
+        left = jnp.concatenate([lesser_buf[0, row], lesser_buf[1, row]], axis=0)
+        imag = other_buf[1, row]
+        right = jnp.concatenate([other_buf[0, row], -imag if first else imag], axis=0)
+        left_spec = jnp.dot(table[...], left, preferred_element_type=jnp.float32)
+        right_spec = jnp.dot(table[...], right, preferred_element_type=jnp.float32)
+        left_real, left_imag = left_spec[:length], left_spec[length:]
+        right_real, right_imag = right_spec[:length], right_spec[length:]
+        if first:
+            real = left_real * right_real + left_imag * right_imag
+            imag = left_imag * right_real - left_real * right_imag
+        else:
+            real = left_real * right_real - left_imag * right_imag
+            imag = left_real * right_imag + left_imag * right_real
+        product = jnp.concatenate([real, imag], axis=0).astype(jnp.bfloat16)
+        result = jnp.dot(table_t[...], product, preferred_element_type=jnp.float32) * scale
+        result = result.astype(jnp.bfloat16)
+        if first:
+            result = jnp.dot(result, volts[...], preferred_element_type=jnp.float32)
+            result = result.astype(jnp.bfloat16)
+        folded[0, row] = result[:count]
+        folded[1, row] = result[count:]
+        return carry
+
+    def work(q, carry):
+        for s in range(len(streams)):
+            def wait_one(k, inner):
+                incoming(s, q, k).wait()
+                return inner
+            lax.fori_loop(1, n, wait_one, 0)
+        lax.fori_loop(q * group, (q + 1) * group, fold, 0)
+
+        def send_one(k, inner):
+            outgoing(q, k).start()
+            return inner
+
+        lax.fori_loop(1, n, send_one, 0)
+        return carry
+
+    lax.fori_loop(0, CHUNKS, work, 0)
+    own_result = pltpu.make_async_copy(
+        folded.at[:, :, pl.ds(me * each, each)], out.at[:, pl.ds(me * rows, rows)], own_out
+    )
+    own_result.start()
+    if first:
+        keeping = pltpu.make_async_copy(lesser_buf, kept, keep)
+        keeping.start()
+
+    def finish(q, carry):
+        def wait_one(k, inner):
+            outgoing(q, k).wait()
+            return inner
+        return lax.fori_loop(1, n, wait_one, carry)
+
+    lax.fori_loop(0, CHUNKS, finish, 0)
+    own_result.wait()
+    if first:
+        keeping.wait()
+
+
+def exchange(n, count, first, scale, operands):
+    two, orbitals, each, width = operands[1].shape
+    rows = orbitals // n
+    hbm = pl.BlockSpec(memory_space=pl.ANY)
+    vmem = pl.BlockSpec(memory_space=pltpu.VMEM)
+    streams = 2 if first else 1
+    out_shape = [jax.ShapeDtypeStruct((2, orbitals, each, width), jnp.bfloat16)]
+    if first:
+        out_shape.append(jax.ShapeDtypeStruct((2, rows, count, width), jnp.bfloat16))
+    buffer = pltpu.VMEM((2, rows, count, width), jnp.bfloat16)
+    dma = pltpu.SemaphoreType.DMA
+    return pl.pallas_call(
+        functools.partial(exchange_kernel, n, count, first, scale),
+        name="polarize" if first else "dress",
+        out_shape=out_shape,
+        in_specs=[hbm, hbm] + [vmem] * (len(operands) - 2),
+        out_specs=[hbm] * len(out_shape),
+        scratch_shapes=[
+            buffer, buffer, buffer,
+            dma((streams, CHUNKS, n)), dma((streams, CHUNKS, n)),
+            dma((CHUNKS, n)), dma((CHUNKS, n)),
+            dma((streams,)), dma, dma,
+        ],
+        compiler_params=pltpu.CompilerParams(
+            collective_id=0 if first else 1, has_side_effects=True, vmem_limit_bytes=VMEM_BYTES
+        ),
+    )(*operands)
+
+
+def per_device(n, g_lesser, g_greater, g_free, coulomb):
+    each, _, orbitals, _ = g_lesser.shape
+    count = n * each
+    if each % 16 or orbitals % (n * CHUNKS):
+        return plain(g_lesser, g_greater, g_free, coulomb)
+    scale = 1.0 / (2 * count * count)
+    full = transform_table(count)
+    table = jnp.asarray(full).astype(jnp.bfloat16)
+    table_t = jnp.asarray(full.T).astype(jnp.bfloat16)
+    lesser = jnp.transpose(g_lesser, (1, 2, 0, 3))
+    greater = jnp.transpose(g_greater, (1, 3, 0, 2))
+    mixed, kept = exchange(n, count, True, scale, (lesser, greater, table, table_t, coulomb))
+    mixed = jnp.transpose(mixed, (0, 2, 1, 3))
+    mixed_real, mixed_imag = mixed[0], mixed[1]
+    square_real = batched(mixed_real, mixed_real) - batched(mixed_imag, mixed_imag)
+    square_imag = batched(mixed_real, mixed_imag) + batched(mixed_imag, mixed_real)
+    inner_real = (mixed_real.astype(jnp.float32) + square_real).astype(jnp.bfloat16)
+    inner_imag = (mixed_imag.astype(jnp.float32) + square_imag).astype(jnp.bfloat16)
+    screen_real = coulomb.astype(jnp.float32)[:, None] + jnp.einsum(
+        "ij,ejk->iek", coulomb, inner_real, preferred_element_type=jnp.float32
+    )
+    screen_imag = jnp.einsum("ij,ejk->iek", coulomb, inner_imag, preferred_element_type=jnp.float32)
+    screen = jnp.stack([screen_real.astype(jnp.bfloat16), screen_imag.astype(jnp.bfloat16)], axis=0)
+    (sigma,) = exchange(n, count, False, scale, (kept, screen, table, table_t))
+    sigma = jnp.transpose(sigma, (0, 2, 1, 3))
+    return dyson(sigma[0], sigma[1], g_free)
 
 
 def solution(mesh):
     return jax.shard_map(
-        per_device,
+        functools.partial(per_device, mesh.shape["ea"]),
         mesh=mesh,
         in_specs=(
             P(("bias", "ea"), None, None, None),

time: 776 us -> 539 us (0.69)
  Pallas kernels: 0 us -> 469 us
  waiting for transfers between devices: 219 us -> 0 us
  blocking collectives: 195 us -> 0 us
  matrix products: 179 us -> 19.2 us
  other arithmetic: 104 us -> 16.5 us
  local copies, waits for them, and re-layouts: 56.6 us -> 33.8 us
  starting transfers between devices: 16.5 us -> 0 us
    pallas_call x0 -> x2, Pallas kernels: none -> 469 us  [exchange(): pl.pallas_call(functools.partial(exchange_kernel, n, count, first, scale)...]
    all_to_all x3 -> x0, waiting for transfers between devices: 219 us -> none  [the longest x1 92.4 us: per_device(): lax.all_to_all(polar_rows, 'ea', split_axis=0, concat_axis=2, tiled=True)]
    all_to_all x2 -> x0, blocking collectives: 195 us -> none  [the longest x1 97.5 us: per_device(): lax.all_to_all(sigma_rows, 'ea', split_axis=0, concat_axis=2, tiled=True)]
    dot_general x12 -> x2, matrix products: 168 us -> 6.67 us  [the longest x1 3.68 us: per_device(): jnp.einsum('ij,ejk->iek', coulomb, inner_real, preferred_element_type=jnp...]
    sub x2 -> x0, other arithmetic: 55.5 us -> none  [complex_mul(): left[0] * right[0] - left[1] * right[1]]
    add x1 -> x0, other arithmetic: 22 us -> none  [complex_mul(): left[0] * right[1] + left[1] * right[0]]
    all_to_all x3 -> x0, starting transfers between devices: 16.5 us -> none  [the longest x1 6.52 us: per_device(): lax.all_to_all(greater_t, 'ea', split_axis=2, concat_axis=0, tiled=True)]
    all_to_all x6 -> x0, local copies, waits for them, and re-layouts: 16.4 us -> none  [the longest x2 5.2 us: per_device(): lax.all_to_all(greater_t, 'ea', split_axis=2, concat_axis=0, tiled=True)]
  transfers between devices with their start and end apart: 3 -> 0, of which waited for: 3 -> 0; matrix products, arithmetic and copies ran while one was open for 7% -> 0% of each run, Pallas kernels for 0% -> 0%
where the time goes in v1:
time: 539 us
  Pallas kernels  469 us (87%)
  local copies, waits for them, and re-layouts  33.8 us (6%)
  matrix products  19.2 us (4%)
  other arithmetic  16.5 us (3%)
    pallas_call x2, Pallas kernels, exchange(): pl.pallas_call(functools.partial(exchange_kernel, n, count, first, scale)...  469 us
    unnamed x10, local copies, waits for them, and re-layouts  16.1 us
    dot_general x12, matrix products, batched(): jnp.einsum('eij,ejk->eik', left, right, preferred_element_type=jnp.float32)  12.5 us

profile of v1, /device:TPU:13, one launch (start us, length us, event | category | flops | bytes accessed | tf_op | source)
XLA Modules:
  0.0 538.6 jit_solution(2294009815102625706)
XLA Ops:
  0.0 6.6 %copy.81 = bf16[16,2,256,256]{3,0,2,1:T(8,128)(2,1)} copy(bf16[16,2,256,256]{3,2,1,0:T(8,128)(2,1)} %param.6) | data formatting | bytes 8388608 | tf_op args[0]
  6.6 7.9 %copy.9 = bf16[16,2,256,256]{2,0,3,1:T(8,128)(2,1)} copy(bf16[16,2,256,256]{3,2,1,0:T(8,128)(2,1)} %param.7) | data formatting | bytes 8388608 | tf_op args[1]
  14.5 280.3 %polarize.1 = (bf16[2,256,16,256]{3,2,1,0:T(8,128)(2,1)}, bf16[2,16,256,256]{3,2,1,0:T(8,128)(2,1)}) custom-call(bf16[2,256,16,256]{3,2,1,0:T(8,128)(2,1)} %bitcast.100, bf16[2,256,16,256]{3,2,1,0:T(8,128)(2,1)} %bitcast.101, bf16[1024,512]{1,0:T(8,128)(2,1)} %constant.9.refs_2_, bf16[512,1024]{1,0:T(8,128)(2,1)} %constant.10.refs_3_, bf16[256,256]{1,0:T(8,128)(2,1)} %refs_4_.1), custom_call_target="tpu_custom_call" | custom-call | tf_op jit(solution)/shard_map/polarize/pallas_call | solution.py:303
  294.8 2.5 slice_bitcast_fusion.3
  297.3 1.4 fusion.38
  298.6 1.4 fusion.42
  300.0 1.4 fusion.34
  301.4 0.0 copy-start.1
  301.4 1.4 fusion.36
  302.7 0.8 copy-done.1
  303.6 0.0 copy-start.3
  303.6 10.7 %fusion.6 = (bf16[16,256,256]{2,0,1:T(8,128)(2,1)S(1)}, bf16[16,256,256]{2,0,1:T(8,128)(2,1)S(1)}) fusion(f32[16,256,256]{2,1,0:T(8,128)S(1)} %fusion.38, f32[16,256,256]{2,1,0:T(8,128)S(1)} %fusion.42, bf16[2,16,256,256]{3,1,2,0:T(8,128)(2,1)S(1)} %bitcast.99, f32[16,256,256]{2,1,0:T(8,128)S(1)} %fusion.34, f32[16,256,256]{2,1,0:T(8,128)S(1)} %fusion.36), kind=kLoop, calls=%fused_computation.15 | loop fusion | flops 8388608 | bytes 25165824 | tf_op jit(solution)/shard_map/convert_element_type | solution.py:337
  314.3 0.0 copy-done.3
  314.3 3.0 fusion.20
  317.3 4.6 copy.13
  321.9 3.7 fusion.22
  325.6 5.5 %copy.11 = f32[16,256,256]{1,0,2:T(8,128)} copy(f32[16,256,256]{2,1,0:T(8,128)} %fusion.22) | data formatting | bytes 8388608 | tf_op jit(solution)/shard_map/ij,ejk->iek/dot_general | solution.py:339
  331.1 0.0 copy-start.2
  331.1 3.1 fusion.7
  334.2 0.0 copy-done.2
  334.2 2.4 pad_maximum_fusion.refs_1_
  336.6 188.7 %dress.1 = bf16[2,256,16,256]{3,2,1,0:T(8,128)(2,1)} custom-call(bf16[2,16,256,256]{3,2,1,0:T(8,128)(2,1)} %get-tuple-element.7.refs_0_, bf16[2,256,16,256]{3,2,1,0:T(8,128)(2,1)} %pad_maximum_fusion.refs_1_, bf16[1024,512]{1,0:T(8,128)(2,1)} %constant.9.refs_2_, bf16[512,1024]{1,0:T(8,128)(2,1)} %constant.10.refs_3_), custom_call_target="tpu_custom_call" | custom-call | tf_op jit(solution)/shard_map/dress/pallas_call | solution.py:303
  525.3 0.0 copy-start
  525.3 2.7 slice_bitcast_fusion
  528.0 0.8 copy-done
  528.7 0.9 fusion.18
  529.6 1.0 subtract_convert_fusion
  530.6 0.9 fusion.10
  531.6 1.0 add_convert_fusion
  532.6 0.7 fusion.16
  533.3 0.9 fusion.28
  534.2 0.7 fusion.13
  534.9 0.9 fusion.31
  535.8 0.4 pad_maximum_fusion.1
  536.2 2.5 copy.27
  (1 shorter events, 0.0 us)
Async XLA Ops:
  301.4 2.2 copy-start.1
  303.6 10.7 %copy-start.3 = (bf16[256,256]{1,0:T(8,128)(2,1)S(1)}, bf16[256,256]{1,0:T(8,128)(2,1)}, u32[]{:S(2)}) copy-start(bf16[256,256]{1,0:T(8,128)(2,1)} %refs_4_.1) | copy-start | bytes 393220
  331.1 3.1 copy-start.2
  525.3 3.5 copy-start

commit v2 on v1

--- a/solution.py
+++ b/solution.py
@@ -318,6 +318,54 @@
     )(*operands)
 
 
+def dot(left, right):
+    return jnp.dot(left, right, preferred_element_type=jnp.float32)
+
+
+def screen_kernel(mixed, volts, out):
+    bare = volts[...]
+    for e in range(mixed.shape[0]):
+        real, imag = mixed[e, 0], mixed[e, 1]
+        square_real = dot(real, real) - dot(imag, imag)
+        square_imag = dot(real, imag) + dot(imag, real)
+        inner_real = (real.astype(jnp.float32) + square_real).astype(jnp.bfloat16)
+        inner_imag = (imag.astype(jnp.float32) + square_imag).astype(jnp.bfloat16)
+        out[e, 0] = (bare.astype(jnp.float32) + dot(bare, inner_real)).astype(jnp.bfloat16)
+        out[e, 1] = dot(bare, inner_imag).astype(jnp.bfloat16)
+
+
+def dyson_kernel(sigma, free, out):
+    for e in range(sigma.shape[0]):
+        real, imag = sigma[e, 0], sigma[e, 1]
+        free_real, free_imag = free[e, 0], free[e, 1]
+        right_real = (dot(real, free_real) - dot(imag, free_imag)).astype(jnp.bfloat16)
+        right_imag = (dot(real, free_imag) + dot(imag, free_real)).astype(jnp.bfloat16)
+        out_real = dot(free_real, right_real) - dot(free_imag, right_imag)
+        out_imag = dot(free_real, right_imag) + dot(free_imag, right_real)
+        out[e, 0] = (free_real.astype(jnp.float32) + out_real).astype(jnp.bfloat16)
+        out[e, 1] = (free_imag.astype(jnp.float32) + out_imag).astype(jnp.bfloat16)
+
+
+def per_energy(kernel, name, matrices, others):
+    each, two, rows, width = matrices.shape
+    block = pl.BlockSpec((2, two, rows, width), lambda i: (i, 0, 0, 0))
+    specs = [block if other.ndim == 4 else pl.BlockSpec(memory_space=pltpu.VMEM) for other in others]
+    products = 6 if name == "screen" else 8
+    return pl.pallas_call(
+        kernel,
+        name=name,
+        grid=(each // 2,),
+        out_shape=jax.ShapeDtypeStruct(matrices.shape, jnp.bfloat16),
+        in_specs=[block] + specs,
+        out_specs=block,
+        cost_estimate=pl.CostEstimate(
+            flops=2 * products * each * rows * rows * width,
+            bytes_accessed=4 * two * each * rows * width,
+            transcendentals=0,
+        ),
+    )(matrices, *others)
+
+
 def per_device(n, g_lesser, g_greater, g_free, coulomb):
     each, _, orbitals, _ = g_lesser.shape
     count = n * each
@@ -330,20 +378,12 @@
     lesser = jnp.transpose(g_lesser, (1, 2, 0, 3))
     greater = jnp.transpose(g_greater, (1, 3, 0, 2))
     mixed, kept = exchange(n, count, True, scale, (lesser, greater, table, table_t, coulomb))
-    mixed = jnp.transpose(mixed, (0, 2, 1, 3))
-    mixed_real, mixed_imag = mixed[0], mixed[1]
-    square_real = batched(mixed_real, mixed_real) - batched(mixed_imag, mixed_imag)
-    square_imag = batched(mixed_real, mixed_imag) + batched(mixed_imag, mixed_real)
-    inner_real = (mixed_real.astype(jnp.float32) + square_real).astype(jnp.bfloat16)
-    inner_imag = (mixed_imag.astype(jnp.float32) + square_imag).astype(jnp.bfloat16)
-    screen_real = coulomb.astype(jnp.float32)[:, None] + jnp.einsum(
-        "ij,ejk->iek", coulomb, inner_real, preferred_element_type=jnp.float32
-    )
-    screen_imag = jnp.einsum("ij,ejk->iek", coulomb, inner_imag, preferred_element_type=jnp.float32)
-    screen = jnp.stack([screen_real.astype(jnp.bfloat16), screen_imag.astype(jnp.bfloat16)], axis=0)
+    mixed = jnp.transpose(mixed, (2, 0, 1, 3))
+    screen = per_energy(screen_kernel, "screen", mixed, (coulomb,))
+    screen = jnp.transpose(screen, (1, 2, 0, 3))
     (sigma,) = exchange(n, count, False, scale, (kept, screen, table, table_t))
-    sigma = jnp.transpose(sigma, (0, 2, 1, 3))
-    return dyson(sigma[0], sigma[1], g_free)
+    sigma = jnp.transpose(sigma, (2, 0, 1, 3))
+    return per_energy(dyson_kernel, "dyson", sigma, (g_free,))
 
 
 def solution(mesh):

time: 539 us -> 524 us (0.972)
  Pallas kernels: 469 us -> 490 us
  matrix products: 19.2 us -> 0 us
  other arithmetic: 16.5 us -> 0 us
    pallas_call x0 -> x2, Pallas kernels: none -> 21.5 us  [per_energy(): pl.pallas_call(kernel, name=name, grid=(each // 2,), out_shape=jax.ShapeD...]
    dot_general x14 -> x0, matrix products: 19.2 us -> none  [the longest x12 12.5 us: batched(): jnp.einsum('eij,ejk->eik', left, right, preferred_element_type=jnp.float32)]
    pallas_call x0 -> x3, local copies, waits for them, and re-layouts: none -> 17.9 us  [the longest x2 11.3 us: exchange(): pl.pallas_call(functools.partial(exchange_kernel, n, count, first, scale)...]
    convert_element_type x2 -> x0, other arithmetic: 10.7 us -> none  [the longest x1 10.7 us: per_device(): (mixed_real.astype(jnp.float32) + square_real).astype(jnp.bfloat16)]
    dot_general x2 -> x0, local copies, waits for them, and re-layouts: 10.1 us -> none  [the longest x1 5.5 us: per_device(): jnp.einsum('ij,ejk->iek', coulomb, inner_real, preferred_element_type=jnp...]
    another operation x3 -> x0, other arithmetic: 5.81 us -> none  [the longest x2 5.43 us: per_device(): jnp.stack([screen_real.astype(jnp.bfloat16), screen_imag.astype(jnp.bfloa...]
    unnamed x10 -> x2, local copies, waits for them, and re-layouts: 16.1 us -> 14.5 us
where the time goes in v2:
time: 524 us; the launch traced here: 523 us
  Pallas kernels  490 us (94%)
  local copies, waits for them, and re-layouts  32.4 us (6%)
    pallas_call x2, Pallas kernels, exchange(): pl.pallas_call(functools.partial(exchange_kernel, n, count, first, scale)...  469 us
    pallas_call x2, Pallas kernels, per_energy(): pl.pallas_call(kernel, name=name, grid=(each // 2,), out_shape=jax.ShapeD...  21.5 us
    unnamed x2, local copies, waits for them, and re-layouts  14.5 us
    pallas_call x2, local copies, waits for them, and re-layouts, exchange(): pl.pallas_call(functools.partial(exchange_kernel, n, count, first, scale)...  11.3 us

profile of v2, /device:TPU:13, one launch (start us, length us, event | category | flops | bytes accessed | tf_op | source)
XLA Modules:
  0.0 522.9 jit_solution(6605690289332231991)
XLA Ops:
  0.0 6.6 %copy.19 = bf16[16,2,256,256]{3,0,2,1:T(8,128)(2,1)} copy(bf16[16,2,256,256]{3,2,1,0:T(8,128)(2,1)} %param.6) | data formatting | bytes 8388608 | tf_op args[0]
  6.6 7.9 %copy.8 = bf16[16,2,256,256]{2,0,3,1:T(8,128)(2,1)} copy(bf16[16,2,256,256]{3,2,1,0:T(8,128)(2,1)} %param.7) | data formatting | bytes 8388608 | tf_op args[1]
  14.5 280.3 %polarize.1 = (bf16[2,256,16,256]{3,2,1,0:T(8,128)(2,1)}, bf16[2,16,256,256]{3,2,1,0:T(8,128)(2,1)}) custom-call(bf16[2,256,16,256]{3,2,1,0:T(8,128)(2,1)} %bitcast.14, bf16[2,256,16,256]{3,2,1,0:T(8,128)(2,1)} %bitcast.15, bf16[1024,512]{1,0:T(8,128)(2,1)} %constant.9.refs_2_, bf16[512,1024]{1,0:T(8,128)(2,1)} %constant.10.refs_3_, bf16[256,256]{1,0:T(8,128)(2,1)} %volts.1), custom_call_target="tpu_custom_call" | custom-call | tf_op jit(solution)/shard_map/polarize/pallas_call | solution.py:303
  294.8 5.7 %copy.18 = bf16[2,256,16,256]{3,1,0,2:T(8,128)(2,1)} copy(bf16[2,256,16,256]{3,2,1,0:T(8,128)(2,1)} %get-tuple-element.8) | data formatting | bytes 8388608 | tf_op jit(solution)/shard_map/polarize/pallas_call | solution.py:303
  300.5 10.2 %screen.1 = bf16[16,2,256,256]{3,2,1,0:T(8,128)(2,1)} custom-call(bf16[16,2,256,256]{3,2,1,0:T(8,128)(2,1)} %bitcast.16, bf16[256,256]{1,0:T(8,128)(2,1)} %volts.1), custom_call_target="tpu_custom_call" | custom-call | flops 3221225472 | bytes 8388608 | tf_op jit(solution)/shard_map/screen/pallas_call | solution.py:354
  310.6 6.6 %copy.17 = bf16[16,2,256,256]{3,0,2,1:T(8,128)(2,1)} copy(bf16[16,2,256,256]{3,2,1,0:T(8,128)(2,1)} %screen.1) | data formatting | bytes 8388608 | tf_op jit(solution)/shard_map/screen/pallas_call | solution.py:354
  317.2 188.7 %dress.1 = bf16[2,256,16,256]{3,2,1,0:T(8,128)(2,1)} custom-call(bf16[2,16,256,256]{3,2,1,0:T(8,128)(2,1)} %get-tuple-element.7.refs_0_, bf16[2,256,16,256]{3,2,1,0:T(8,128)(2,1)} %bitcast.13, bf16[1024,512]{1,0:T(8,128)(2,1)} %constant.9.refs_2_, bf16[512,1024]{1,0:T(8,128)(2,1)} %constant.10.refs_3_), custom_call_target="tpu_custom_call" | custom-call | tf_op jit(solution)/shard_map/dress/pallas_call | solution.py:303
  505.9 5.6 %copy.16 = bf16[2,256,16,256]{3,1,0,2:T(8,128)(2,1)} copy(bf16[2,256,16,256]{3,2,1,0:T(8,128)(2,1)} %dress.1) | data formatting | bytes 8388608 | tf_op jit(solution)/shard_map/dress/pallas_call | solution.py:303
  511.5 11.3 %dyson.1 = bf16[16,2,256,256]{3,2,1,0:T(8,128)(2,1)} custom-call(bf16[16,2,256,256]{3,2,1,0:T(8,128)(2,1)} %bitcast.17, bf16[16,2,256,256]{3,2,1,0:T(8,128)(2,1)} %free.1), custom_call_target="tpu_custom_call" | custom-call | flops 4294967296 | bytes 8388608 | tf_op jit(solution)/shard_map/dyson/pallas_call | solution.py:354

commit v3 on v2

--- a/solution.py
+++ b/solution.py
@@ -135,6 +135,7 @@
 
 MESH = pl.DeviceIdType.MESH
 CHUNKS = 4
+LANES = 128
 VMEM_BYTES = 60 * 1024 * 1024
 
 
@@ -165,8 +166,9 @@
 ):
     if first:
         (lesser, other, table, table_t, volts, out, kept,
-         lesser_buf, other_buf, folded, in_send, in_recv, out_send, out_recv, own_in, own_out, keep) = refs
-        streams = ((lesser, lesser_buf), (other, other_buf))
+         lesser_buf, other_buf, folded, in_send, in_recv, out_send, out_recv, own_in, own_out, keep,
+         lesser_raw, other_raw, lesser_rows, other_rows) = refs
+        streams = ((lesser_rows, lesser_buf), (other_rows, other_buf))
     else:
         (kept, other, table, table_t, out,
          lesser_buf, other_buf, folded, in_send, in_recv, out_send, out_recv, own_in, own_out, keep) = refs
@@ -207,24 +209,59 @@
             own_in.at[s],
         )
 
-    if not first:
+    def send_chunk(s, q):
+        def send_one(k, inner):
+            incoming(s, q, k).start()
+            return inner
+
+        lax.fori_loop(1, n, send_one, 0)
+
+    if first:
+        raw = (
+            pltpu.make_async_copy(lesser, lesser_raw, own_in.at[0]),
+            pltpu.make_async_copy(other, other_raw, own_in.at[1]),
+        )
+        for copy in raw:
+            copy.start()
+        greet(n)
+        raw[0].wait()
+        mine = pl.ds(pl.multiple_of(me * each, each), each)
+
+        def regroup(k, carry):
+            peer = lax.rem(me + k, n)
+            block = pl.ds(pl.multiple_of(peer * rows, rows), rows)
+            for c in range(2):
+                lesser_rows[c, block] = jnp.swapaxes(lesser_raw[:, c, block, :], 0, 1)
+            return carry
+
+        def regroup_and_send(k, carry):
+            regroup(k, carry)
+
+            def send_one(q, inner):
+                incoming(0, q, k).start()
+                return inner
+
+            return lax.fori_loop(0, CHUNKS, send_one, carry)
+
+        lax.fori_loop(1, n, regroup_and_send, 0)
+        regroup(0, 0)
+        raw[1].wait()
+        for low in range(0, rows * n, LANES):
+            for c in range(2):
+                turned = jnp.stack(
+                    [other_raw[e, c, :, low : low + LANES].T for e in range(each)], axis=0
+                )
+                other_rows[c, low : low + LANES] = jnp.swapaxes(turned, 0, 1)
+        lax.fori_loop(0, CHUNKS, lambda q, carry: (send_chunk(1, q), carry)[1], 0)
+        for source, target in streams:
+            for c in range(2):
+                target[c, :, mine, :] = source[c, pl.ds(me * rows, rows)]
+    else:
         pltpu.make_async_copy(kept, lesser_buf, keep).start()
-    for s in range(len(streams)):
-        own_incoming(s).start()
-    greet(n)
-
-    def send_chunk(q, carry):
-        for s in range(len(streams)):
-            def send_one(k, inner):
-                incoming(s, q, k).start()
-                return inner
-            lax.fori_loop(1, n, send_one, 0)
-        return carry
-
-    lax.fori_loop(0, CHUNKS, send_chunk, 0)
-    for s in range(len(streams)):
-        own_incoming(s).wait()
-    if not first:
+        own_incoming(0).start()
+        greet(n)
+        lax.fori_loop(0, CHUNKS, lambda q, carry: (send_chunk(0, q), carry)[1], 0)
+        own_incoming(0).wait()
         pltpu.make_async_copy(kept, lesser_buf, keep).wait()
 
     length = 2 * count
@@ -290,7 +327,8 @@
 
 
 def exchange(n, count, first, scale, operands):
-    two, orbitals, each, width = operands[1].shape
+    orbitals, width = operands[1].shape[-3 if not first else -2], operands[1].shape[-1]
+    each = count // n
     rows = orbitals // n
     hbm = pl.BlockSpec(memory_space=pl.ANY)
     vmem = pl.BlockSpec(memory_space=pltpu.VMEM)
@@ -300,6 +338,10 @@
         out_shape.append(jax.ShapeDtypeStruct((2, rows, count, width), jnp.bfloat16))
     buffer = pltpu.VMEM((2, rows, count, width), jnp.bfloat16)
     dma = pltpu.SemaphoreType.DMA
+    staging = []
+    if first:
+        staging = [pltpu.VMEM((each, 2, orbitals, width), jnp.bfloat16)] * 2
+        staging += [pltpu.VMEM((2, orbitals, each, width), jnp.bfloat16)] * 2
     return pl.pallas_call(
         functools.partial(exchange_kernel, n, count, first, scale),
         name="polarize" if first else "dress",
@@ -311,7 +353,7 @@
             dma((streams, CHUNKS, n)), dma((streams, CHUNKS, n)),
             dma((CHUNKS, n)), dma((CHUNKS, n)),
             dma((streams,)), dma, dma,
-        ],
+        ] + staging,
         compiler_params=pltpu.CompilerParams(
             collective_id=0 if first else 1, has_side_effects=True, vmem_limit_bytes=VMEM_BYTES
         ),
@@ -369,15 +411,13 @@
 def per_device(n, g_lesser, g_greater, g_free, coulomb):
     each, _, orbitals, _ = g_lesser.shape
     count = n * each
-    if each % 16 or orbitals % (n * CHUNKS):
+    if each % 16 or orbitals % (n * 16) or orbitals % LANES:
         return plain(g_lesser, g_greater, g_free, coulomb)
     scale = 1.0 / (2 * count * count)
     full = transform_table(count)
     table = jnp.asarray(full).astype(jnp.bfloat16)
     table_t = jnp.asarray(full.T).astype(jnp.bfloat16)
-    lesser = jnp.transpose(g_lesser, (1, 2, 0, 3))
-    greater = jnp.transpose(g_greater, (1, 3, 0, 2))
-    mixed, kept = exchange(n, count, True, scale, (lesser, greater, table, table_t, coulomb))
+    mixed, kept = exchange(n, count, True, scale, (g_lesser, g_greater, table, table_t, coulomb))
     mixed = jnp.transpose(mixed, (2, 0, 1, 3))
     screen = per_energy(screen_kernel, "screen", mixed, (coulomb,))
     screen = jnp.transpose(screen, (1, 2, 0, 3))

time: 524 us -> 509 us (0.971)
  local copies, waits for them, and re-layouts: 32.4 us -> 17.9 us
    unnamed x2 -> x0, local copies, waits for them, and re-layouts: 14.5 us -> none
where the time goes in v3:
time: 509 us
  Pallas kernels  491 us (96%)
  local copies, waits for them, and re-layouts  17.9 us (4%)
    pallas_call x2, Pallas kernels, exchange(): pl.pallas_call(functools.partial(exchange_kernel, n, count, first, scale)...  469 us
    pallas_call x2, Pallas kernels, per_energy(): pl.pallas_call(kernel, name=name, grid=(each // 2,), out_shape=jax.ShapeD...  21.5 us
    pallas_call x2, local copies, waits for them, and re-layouts, exchange(): pl.pallas_call(functools.partial(exchange_kernel, n, count, first, scale)...  11.3 us

profile of v3, /device:TPU:13, one launch (start us, length us, event | category | flops | bytes accessed | tf_op | source)
XLA Modules:
  0.0 508.7 jit_solution(4826903949875256365)
XLA Ops:
  0.0 281.9 %polarize.1 = (bf16[2,256,16,256]{3,2,1,0:T(8,128)(2,1)}, bf16[2,16,256,256]{3,2,1,0:T(8,128)(2,1)}) custom-call(bf16[16,2,256,256]{3,2,1,0:T(8,128)(2,1)} %refs_0_.1, bf16[16,2,256,256]{3,2,1,0:T(8,128)(2,1)} %refs_1_.1, bf16[1024,512]{1,0:T(8,128)(2,1)} %constant.9.refs_2_, bf16[512,1024]{1,0:T(8,128)(2,1)} %constant.10.refs_3_, bf16[256,256]{1,0:T(8,128)(2,1)} %volts.1), custom_call_target="tpu_custom_call" | custom-call | tf_op jit(solution)/shard_map/polarize/pallas_call | solution.py:345
  281.9 5.7 %copy.15 = bf16[2,256,16,256]{3,1,0,2:T(8,128)(2,1)} copy(bf16[2,256,16,256]{3,2,1,0:T(8,128)(2,1)} %get-tuple-element.8) | data formatting | bytes 8388608 | tf_op jit(solution)/shard_map/polarize/pallas_call | solution.py:345
  287.6 10.2 %screen.1 = bf16[16,2,256,256]{3,2,1,0:T(8,128)(2,1)} custom-call(bf16[16,2,256,256]{3,2,1,0:T(8,128)(2,1)} %bitcast.10, bf16[256,256]{1,0:T(8,128)(2,1)} %volts.1), custom_call_target="tpu_custom_call" | custom-call | flops 3221225472 | bytes 8388608 | tf_op jit(solution)/shard_map/screen/pallas_call | solution.py:396
  297.8 6.6 %copy.14 = bf16[16,2,256,256]{3,0,2,1:T(8,128)(2,1)} copy(bf16[16,2,256,256]{3,2,1,0:T(8,128)(2,1)} %screen.1) | data formatting | bytes 8388608 | tf_op jit(solution)/shard_map/screen/pallas_call | solution.py:396
  304.4 187.4 %dress.1 = bf16[2,256,16,256]{3,2,1,0:T(8,128)(2,1)} custom-call(bf16[2,16,256,256]{3,2,1,0:T(8,128)(2,1)} %get-tuple-element.7.refs_0_, bf16[2,256,16,256]{3,2,1,0:T(8,128)(2,1)} %bitcast.9, bf16[1024,512]{1,0:T(8,128)(2,1)} %constant.9.refs_2_, bf16[512,1024]{1,0:T(8,128)(2,1)} %constant.10.refs_3_), custom_call_target="tpu_custom_call" | custom-call | tf_op jit(solution)/shard_map/dress/pallas_call | solution.py:345
  491.8 5.6 %copy.13 = bf16[2,256,16,256]{3,1,0,2:T(8,128)(2,1)} copy(bf16[2,256,16,256]{3,2,1,0:T(8,128)(2,1)} %dress.1) | data formatting | bytes 8388608 | tf_op jit(solution)/shard_map/dress/pallas_call | solution.py:345
  497.4 11.3 %dyson.1 = bf16[16,2,256,256]{3,2,1,0:T(8,128)(2,1)} custom-call(bf16[16,2,256,256]{3,2,1,0:T(8,128)(2,1)} %bitcast.11, bf16[16,2,256,256]{3,2,1,0:T(8,128)(2,1)} %free.1), custom_call_target="tpu_custom_call" | custom-call | flops 4294967296 | bytes 8388608 | tf_op jit(solution)/shard_map/dyson/pallas_call | solution.py:396
